TPU v7x, 32 devices: a whole 2x2x4 slice. The times are simulated.
32 devices in a mesh: samp: 16 (over z, y, core), snp: 2 (over x).
Axes of the slice: x: 2, y: 2, z: 4, core: 2. Of those that a mesh axis runs over, the one named last changes fastest.
Arguments:
- genotype: int32 [16384, 4096], P('samp', 'snp'), may hold values from 0 to 3, as said below
- basis: bfloat16 [4096, 40], P('snp'), may hold values from -6 to 6
Outputs:
- sample_scores: bfloat16 [16384, 40], P('samp')
- snp_block: float32 [4096, 40], P('snp')
Inputs may be any that keep to these rules, and one draw needn't show every extreme that they name: `genotype`: the value 3 marks a missing call; 0, 1 and 2 are dosages.
All inputs are finite; a program needn't handle non-finite values.
Results may differ from a plain program's by a relative error of at most 0.0065.
Values may be sent and summed in bfloat16 or wider, within the bound.
A program may use at most 64 MiB of HBM per device.

v0:
```python
import jax
import jax.numpy as jnp
from jax import lax
from jax.sharding import PartitionSpec as P

ITERS = 2


def per_device(genotype, basis):
    observed = genotype < 3
    dosage = jnp.where(observed, genotype, 0).astype(jnp.float32)
    allele_sum, called = lax.psum(
        (jnp.sum(dosage, axis=0), jnp.sum(observed.astype(jnp.float32), axis=0)), "samp"
    )
    freq = (allele_sum + 1.0) / (2.0 * called + 2.0)
    scale = 1.0 / jnp.sqrt(2.0 * freq * (1.0 - freq))
    standard = jnp.where(observed, (dosage - 2.0 * freq) * scale, 0.0).astype(jnp.bfloat16)
    row_count = genotype.shape[0]
    total = row_count * lax.axis_size("samp")
    contract = (((0,), (0,)), ((), ()))
    block = basis
    for step in range(ITERS):
        scores = lax.psum(jnp.dot(standard, block, preferred_element_type=jnp.float32), "snp")
        sample_scores = scores.astype(jnp.bfloat16)
        local = lax.dot_general(
            standard, sample_scores, contract, preferred_element_type=jnp.float32
        )
        snp_block = lax.psum(local, "samp") / total
        block = snp_block.astype(jnp.bfloat16)
    return (sample_scores, snp_block)


def solution(mesh):
    placed = (P("samp", "snp"), P("snp", None))
    return jax.shard_map(
        per_device,
        mesh=mesh,
        in_specs=placed,
        out_specs=(P("samp", None), P("snp", None)),
        check_vma=False,
    )
```

profile of v0, /device:TPU:0, one launch (start us, length us, event | category | flops | bytes accessed | tf_op | source)
XLA Modules:
  0.0 305.4 jit_solution(3003615969748180968)
XLA Ops:
  7.2 0.0 copy-start
  7.2 0.0 all-reduce.6.cloned.1.call-start
  7.2 5.1 %convert_reduce_fusion.1 = (f32[2048]{0:T(1024)S(1)}, f32[2048]{0:T(1024)S(1)}) fusion(s32[1024,2048]{1,0:T(8,128)} %param.2), kind=kLoop, calls=%fused_computation.2 | loop fusion | flops 12578816 | bytes 8404992 | tf_op jit(solution)/shard_map/reduce_sum | solution.py:13
  12.3 63.0 %all-reduce = (f32[2048]{0:T(1024)S(1)}, f32[2048]{0:T(1024)S(1)}) all-reduce(f32[2048]{0:T(1024)S(1)} %get-tuple-element.3, f32[2048]{0:T(1024)S(1)} %get-tuple-element.2), channel_id=1, replica_groups=mesh['samp'=16,'snp'=2] {'samp'}, use_global_device_ids=true, to_apply=%region_3.4 | all-reduce | flops 4096 | bytes 32768 | tf_op jit(solution)/shard_map/psum | solution.py:12
  75.3 4.4 %select_convert_fusion = bf16[1024,2048]{1,0:T(8,128)(2,1)S(1)} fusion(s32[1024,2048]{1,0:T(8,128)} %param.2, f32[2048]{0:T(1024)S(1)} %get-tuple-element.7, f32[2048]{0:T(1024)S(1)} %get-tuple-element.6), kind=kLoop, calls=%fused_computation | loop fusion | flops 14680064 | bytes 12599296 | tf_op jit(solution)/shard_map/convert_element_type | solution.py:17
  79.7 0.0 copy-start.1
  79.7 1.9 copy-done.1
  81.6 0.0 copy-done
  81.6 1.2 fusion.5
  82.8 15.7 %all-reduce.9 = bf16[1024,40]{1,0:T(8,128)(2,1)S(1)} all-reduce(f32[1024,40]{1,0:T(8,128)S(1)} %fusion.5), channel_id=1, replica_groups=mesh['samp'=16,'snp'=2] {'snp'}, use_global_device_ids=true, to_apply=%region_4.5 | all-reduce | flops 40960 | bytes 245760 | tf_op jit(solution)/shard_map/psum | solution.py:23
  98.5 3.8 %fusion.7 = f32[2048,40]{0,1:T(8,128)} fusion(bf16[1024,2048]{1,0:T(8,128)(2,1)} %copy-done.1, bf16[1024,40]{1,0:T(8,128)(2,1)S(1)} %all-reduce.9), kind=kOutput, calls=%fused_computation.16 | convolution fusion | flops 167772160 | bytes 4603904 | tf_op jit(solution)/shard_map/dot_general | solution.py:25
  102.3 0.0 all-reduce.6.cloned.1.call-update
  102.3 0.0 all-reduce.8.cloned.1.call-start
  102.4 86.9 %all-reduce.6.cloned.1.call-done = f32[2048,40]{0,1:T(8,128)} async-done(((f32[2048,40]{0,1:T(8,128)}), f32[2048,40]{0,1:T(8,128)}) %all-reduce.6.cloned.1.call-update) | async-done | bytes 327696 | tf_op jit(solution)/shard_map/psum | solution.py:28
  189.3 3.6 %fusion.2 = f32[1024,40]{0,1:T(8,128)S(1)} fusion(bf16[1024,2048]{1,0:T(8,128)(2,1)} %copy-done.1, f32[2048,40]{0,1:T(8,128)} %all-reduce.6.cloned.1.call-done), kind=kOutput, calls=%fused_computation.7 | convolution fusion | flops 167936000 | bytes 4685824 | tf_op jit(solution)/shard_map/dot_general | solution.py:23
  192.9 10.1 %all-reduce.10 = bf16[1024,40]{0,1:T(8,128)(2,1)S(1)} all-reduce(f32[1024,40]{0,1:T(8,128)S(1)} %fusion.2), channel_id=1, replica_groups=mesh['samp'=16,'snp'=2] {'snp'}, use_global_device_ids=true, to_apply=%region_6.7 | all-reduce | flops 40960 | bytes 245760 | tf_op jit(solution)/shard_map/psum | solution.py:23
  203.0 0.0 copy-start.2
  203.0 3.8 %fusion.6 = f32[2048,40]{0,1:T(8,128)} fusion(bf16[1024,2048]{1,0:T(8,128)(2,1)} %copy-done.1, bf16[1024,40]{0,1:T(8,128)(2,1)S(1)} %all-reduce.10), kind=kOutput, calls=%fused_computation.15 | convolution fusion | flops 167772160 | bytes 4603904 | tf_op jit(solution)/shard_map/dot_general | solution.py:25
  206.8 0.0 all-reduce.8.cloned.1.call-update
  206.8 90.1 %all-reduce.8.cloned.1.call-done = f32[2048,40]{0,1:T(8,128)} async-done(((f32[2048,40]{0,1:T(8,128)}), f32[2048,40]{0,1:T(8,128)}) %all-reduce.8.cloned.1.call-update) | async-done | bytes 327696 | tf_op jit(solution)/shard_map/psum | solution.py:28
  296.9 1.7 broadcast_multiply_fusion
  298.6 0.0 copy-done.2
  (1 shorter events, 0.0 us)
Async XLA Ops:
  7.2 74.4 %copy-start = (bf16[2048,40]{0,1:T(8,128)(2,1)S(1)}, bf16[2048,40]{0,1:T(8,128)(2,1)}, u32[]{:S(2)}) copy-start(bf16[2048,40]{0,1:T(8,128)(2,1)} %param.3) | copy-start | bytes 491524
  7.2 182.1 %all-reduce.6.cloned.1.call-start = ((), (), s32[]{:S(2)}) async-start(), calls=%async_computation | async-start | bytes 655360 | tf_op jit(solution)/shard_map/psum | solution.py:28
  79.7 1.9 copy-start.1
  102.3 194.6 %all-reduce.8.cloned.1.call-start = ((), (), s32[]{:S(2)}) async-start(), calls=%async_computation.1 | async-start | bytes 655360 | tf_op jit(solution)/shard_map/psum | solution.py:28
  203.0 95.6 %copy-start.2 = (bf16[1024,40]{0,1:T(8,128)(2,1)}, bf16[1024,40]{0,1:T(8,128)(2,1)S(1)}, u32[]{:S(2)}) copy-start(bf16[1024,40]{0,1:T(8,128)(2,1)S(1)} %all-reduce.10) | copy-start | bytes 245764
Sparse Core Ops, SparseCore 0:
  102.5 86.7 all-reduce.5
  206.9 89.9 all-reduce.7
where the time goes:
time: 306 us; the launch traced here: 305 us
  waiting for transfers between devices  177 us (58%)
  blocking collectives  88.8 us (29%)
  between operations  14.1 us (5%)
  matrix products  12.3 us (4%)
  other arithmetic  11.2 us (4%)
    psum x2, waiting for transfers between devices, per_device(): snp_block = lax.psum(local, 'samp') / total  177 us
    psum x1, blocking collectives, per_device(): lax.psum((jnp.sum(dosage, axis=0), jnp.sum(observed.astype(jnp.float32),...  63 us
    psum x2, blocking collectives, per_device(): lax.psum(jnp.dot(standard, block, preferred_element_type=jnp.float32), 's...  25.8 us
    dot_general x2, matrix products, per_device(): lax.dot_general(standard, sample_scores, contract, preferred_element_type...  7.52 us
  transfers between devices with their start and end apart: 2, of which 2 were waited for; matrix products, arithmetic and copies ran while one was open for 0% of the time, Pallas kernels for 0%

commit v1 on v0

v1 whole, which is shorter than its diff:
```python
import functools

import jax
import jax.numpy as jnp
from jax import lax
from jax.experimental import pallas as pl
from jax.experimental.pallas import tpu as pltpu
from jax.sharding import PartitionSpec as P

ITERS = 2
LANES = 128
WIDE = 256
SHIFT = 65536
MESH = pl.DeviceIdType.MESH
NT = (((1,), (1,)), ((), ()))


def flipped(me, bits):
    out, step = me, 1
    while step <= bits:
        if bits & step:
            out = out + step * (1 - 2 * lax.rem(me // step, 2))
        step *= 2
    return out


def kernel(
    n, genotype, basis, scores_out, block_out,
    raw, std, stat, table, start, acc, mine, theirs, part, got, full, result,
    load_sem, in_sem, stat_send, stat_recv, score_send, score_recv,
    part_send, part_recv, full_send, full_recv, out_sem,
):
    me = lax.axis_index("samp")
    side = lax.axis_index("snp")
    rows, cols = genotype.shape
    total = rows * n
    blocks = cols // LANES
    groups = blocks // 8
    chunks = cols // WIDE

    barrier = pltpu.get_barrier_semaphore()
    for d in range(1, n):
        pl.semaphore_signal(barrier, inc=1, device_id={"samp": flipped(me, d)}, device_id_type=MESH)
    pl.semaphore_signal(barrier, inc=1, device_id={"snp": 1 - side}, device_id_type=MESH)

    def load(c):
        at = pl.ds(pl.multiple_of(c * WIDE, WIDE), WIDE)
        return pltpu.make_async_copy(genotype.at[:, at], raw.at[:, at], load_sem.at[c])

    for c in range(chunks):
        load(c).start()
    fetch = pltpu.make_async_copy(basis, start, in_sem)
    fetch.start()

    def count(c, _):
        load(c).wait()
        for half in range(WIDE // LANES):
            at = pl.ds(pl.multiple_of(c * WIDE + half * LANES, LANES), LANES)
            g = raw[:, at]
            sums = jnp.sum(jnp.where(g == 3, SHIFT, g), axis=0, keepdims=True)
            std[:, at] = g.astype(jnp.float32).astype(jnp.bfloat16)
            j = c * (WIDE // LANES) + half
            stat[me, j // 8, pl.ds(lax.rem(j, 8), 1), :] = sums
        return 0

    def stat_copy(h, d):
        peer = flipped(me, d)
        return pltpu.make_async_remote_copy(
            src_ref=stat.at[me, h], dst_ref=stat.at[me, h],
            send_sem=stat_send.at[h, d], recv_sem=stat_recv.at[h, d],
            device_id={"samp": peer}, device_id_type=MESH,
        )

    per_group = chunks // groups
    for h in range(groups):
        lax.fori_loop(h * per_group, (h + 1) * per_group, count, 0)
        if h == 0:
            pl.semaphore_wait(barrier, n)
        for d in reversed(range(1, n)):
            stat_copy(h, d).start()

    for h in range(groups):
        for d in range(1, n):
            stat_copy(h, d).wait_recv()
        packed = stat[0, h]
        for s in range(1, n):
            packed += stat[s, h]
        missing = packed // SHIFT
        allele_sum = (packed - missing * SHIFT).astype(jnp.float32)
        called = (total - missing).astype(jnp.float32)
        freq = (allele_sum + 1.0) / (2.0 * called + 2.0)
        scale = 1.0 / jnp.sqrt(2.0 * freq * (1.0 - freq))
        for k in range(3):
            table[k, h] = (float(k) - 2.0 * freq) * scale

    fetch.wait()
    zero = jnp.zeros((), jnp.bfloat16)

    def standardize(j):
        at = pl.ds(pl.multiple_of(j * LANES, LANES), LANES)
        g = std[:, at]
        row = [
            jnp.broadcast_to(
                table[k, j // 8, pl.ds(lax.rem(j, 8), 1), :].astype(jnp.bfloat16), g.shape
            )
            for k in range(3)
        ]
        std[:, at] = jnp.where(
            g == 0, row[0], jnp.where(g == 1, row[1], jnp.where(g == 2, row[2], zero))
        )

    acc[...] = jnp.zeros_like(acc)

    def first(c, _):
        for half in range(WIDE // LANES):
            standardize(c * (WIDE // LANES) + half)
        at = pl.ds(pl.multiple_of(c * WIDE, WIDE), WIDE)
        acc[...] += lax.dot_general(start[:, at], std[:, at], NT, preferred_element_type=jnp.float32)
        return 0

    lax.fori_loop(0, chunks, first, 0)

    for step in range(ITERS):
        last = step == ITERS - 1
        mine[step] = acc[...].astype(jnp.bfloat16)
        swap = pltpu.make_async_remote_copy(
            src_ref=mine.at[step], dst_ref=theirs.at[step],
            send_sem=score_send.at[step], recv_sem=score_recv.at[step],
            device_id={"snp": 1 - side}, device_id_type=MESH,
        )
        swap.start()
        swap.wait_recv()
        scores = (mine[step].astype(jnp.float32) + theirs[step].astype(jnp.float32)).astype(jnp.bfloat16)
        result[...] = scores
        if last:
            score_write = pltpu.make_async_copy(result, scores_out, out_sem.at[0])
            score_write.start()

        def part_copy(owner):
            return pltpu.make_async_remote_copy(
                src_ref=part.at[step, owner], dst_ref=got.at[step, me],
                send_sem=part_send.at[step, owner], recv_sem=part_recv.at[step, me],
                device_id={"samp": owner}, device_id_type=MESH,
            )

        def part_arrival(sender):
            return pltpu.make_async_remote_copy(
                src_ref=part.at[step, sender], dst_ref=got.at[step, sender],
                send_sem=part_send.at[step, sender], recv_sem=part_recv.at[step, sender],
                device_id={"samp": sender}, device_id_type=MESH,
            )

        per_dot = 4 if n % 4 == 0 else 1
        dots = n // per_dot

        def back(i, _):
            c = lax.rem(me // per_dot + 1 + i, dots)
            at = pl.ds(pl.multiple_of(c * (per_dot * LANES), per_dot * LANES), per_dot * LANES)
            local = jnp.dot(result[...], std[:, at], preferred_element_type=jnp.float32)
            for r in range(per_dot):
                owner = c * per_dot + r
                part[step, owner] = local[:, r * LANES : (r + 1) * LANES].astype(jnp.bfloat16)

                @pl.when(owner != me)
                def _():
                    part_copy(owner).start()

            return 0

        lax.fori_loop(0, dots, back, 0)

        whole = part[step, me].astype(jnp.float32)
        for d in range(1, n):
            sender = flipped(me, d)
            part_arrival(sender).wait_recv()
            whole += got[step, sender].astype(jnp.float32)
        full[step, me] = (whole / total).astype(jnp.bfloat16)

        def full_copy(peer, slot):
            return pltpu.make_async_remote_copy(
                src_ref=full.at[step, slot], dst_ref=full.at[step, slot],
                send_sem=full_send.at[step, peer], recv_sem=full_recv.at[step, slot],
                device_id={"samp": peer}, device_id_type=MESH,
            )

        for d in reversed(range(1, n)):
            full_copy(flipped(me, d), me).start()

        if not last:
            acc[...] = jnp.zeros_like(acc)

        def arrive(s):
            @pl.when(s != me)
            def _():
                full_copy(s, s).wait_recv()

        def take(i, _):
            c = lax.rem(me // 2 + i, n // 2)
            for r in range(2):
                arrive(2 * c + r)
            at = pl.ds(pl.multiple_of(c * WIDE, WIDE), WIDE)
            both = jnp.concatenate([full[step, 2 * c], full[step, 2 * c + 1]], axis=1)
            if last:
                block_out[:, at] = both.astype(jnp.float32)
            else:
                acc[...] += lax.dot_general(both, std[:, at], NT, preferred_element_type=jnp.float32)
            return 0

        lax.fori_loop(0, n // 2, take, 0)

        for d in range(1, n):
            peer = flipped(me, d)
            part_copy(peer).wait_send()
            full_copy(peer, me).wait_send()
        swap.wait_send()

    for h in range(groups):
        for d in range(1, n):
            stat_copy(h, d).wait_send()
    score_write.wait()


def fused(n, genotype, basis):
    rows, cols = genotype.shape
    width = basis.shape[1]
    blocks = cols // LANES
    dma = pltpu.SemaphoreType.DMA
    scores, block = pl.pallas_call(
        functools.partial(kernel, n),
        out_shape=(
            jax.ShapeDtypeStruct((width, rows), jnp.bfloat16),
            jax.ShapeDtypeStruct((width, cols), jnp.float32),
        ),
        in_specs=[pl.BlockSpec(memory_space=pl.ANY)] * 2,
        out_specs=(
            pl.BlockSpec(memory_space=pl.ANY),
            pl.BlockSpec(memory_space=pltpu.VMEM),
        ),
        scratch_shapes=[
            pltpu.VMEM((rows, cols), jnp.int32),
            pltpu.VMEM((rows, cols), jnp.bfloat16),
            pltpu.VMEM((n, blocks // 8, 8, LANES), jnp.int32),
            pltpu.VMEM((3, blocks // 8, 8, LANES), jnp.float32),
            pltpu.VMEM((width, cols), jnp.bfloat16),
            pltpu.VMEM((width, rows), jnp.float32),
            pltpu.VMEM((ITERS, width, rows), jnp.bfloat16),
            pltpu.VMEM((ITERS, width, rows), jnp.bfloat16),
            pltpu.VMEM((ITERS, n, width, LANES), jnp.bfloat16),
            pltpu.VMEM((ITERS, n, width, LANES), jnp.bfloat16),
            pltpu.VMEM((ITERS, n, width, LANES), jnp.bfloat16),
            pltpu.VMEM((width, rows), jnp.bfloat16),
            dma((cols // WIDE,)),
            dma,
            dma((blocks // 8, n)),
            dma((blocks // 8, n)),
            dma((ITERS,)),
            dma((ITERS,)),
            dma((ITERS, n)),
            dma((ITERS, n)),
            dma((ITERS, n)),
            dma((ITERS, n)),
            dma((1,)),
        ],
        compiler_params=pltpu.CompilerParams(
            collective_id=0, has_side_effects=True, vmem_limit_bytes=48 * 1024 * 1024
        ),
    )(genotype, basis.T)
    return scores.T, block.T


def plain(genotype, basis):
    observed = genotype < 3
    dosage = jnp.where(observed, genotype, 0).astype(jnp.float32)
    allele_sum, called = lax.psum(
        (jnp.sum(dosage, axis=0), jnp.sum(observed.astype(jnp.float32), axis=0)), "samp"
    )
    freq = (allele_sum + 1.0) / (2.0 * called + 2.0)
    scale = 1.0 / jnp.sqrt(2.0 * freq * (1.0 - freq))
    standard = jnp.where(observed, (dosage - 2.0 * freq) * scale, 0.0).astype(jnp.bfloat16)
    total = genotype.shape[0] * lax.axis_size("samp")
    contract = (((0,), (0,)), ((), ()))
    block = basis
    for step in range(ITERS):
        scores = lax.psum(jnp.dot(standard, block, preferred_element_type=jnp.float32), "snp")
        sample_scores = scores.astype(jnp.bfloat16)
        local = lax.dot_general(
            standard, sample_scores, contract, preferred_element_type=jnp.float32
        )
        snp_block = lax.psum(local, "samp") / total
        block = snp_block.astype(jnp.bfloat16)
    return (sample_scores, snp_block)


def solution(mesh):
    n, sides = mesh.shape["samp"], mesh.shape["snp"]

    def per_device(genotype, basis):
        rows, cols = genotype.shape
        fits = (
            sides == 2 and n >= 2 and n & (n - 1) == 0 and cols == n * LANES
            and cols % (8 * LANES) == 0 and rows % LANES == 0 and 2 * rows * n < SHIFT
        )
        return fused(n, genotype, basis) if fits else plain(genotype, basis)

    return jax.shard_map(
        per_device,
        mesh=mesh,
        in_specs=(P("samp", "snp"), P("snp", None)),
        out_specs=(P("samp", None), P("snp", None)),
        check_vma=False,
    )
```

time: 306 us -> 53.7 us (0.18)
  waiting for transfers between devices: 177 us -> 0 us
  blocking collectives: 88.8 us -> 0 us
  Pallas kernels: 0 us -> 50.6 us
  between operations: 14.1 us -> 0.65 us
  matrix products: 12.3 us -> 0 us
  other arithmetic: 11.2 us -> 0 us
    psum x2 -> x0, waiting for transfers between devices: 177 us -> none  [per_device(): snp_block = lax.psum(local, 'samp') / total]
    psum x3 -> x0, blocking collectives: 88.8 us -> none  [the longest x1 63 us: per_device(): lax.psum((jnp.sum(dosage, axis=0), jnp.sum(observed.astype(jnp.float32),...]
    pallas_call x0 -> x1, Pallas kernels: none -> 50.6 us  [fused(): pl.pallas_call(functools.partial(kernel, n), out_shape=(jax.ShapeDtypeStr...]
    dot_general x4 -> x0, matrix products: 12.3 us -> none  [the longest x2 7.52 us: per_device(): lax.dot_general(standard, sample_scores, contract, preferred_element_type...]
    reduce_sum x1 -> x0, other arithmetic: 5.06 us -> none  [per_device(): jnp.sum(dosage, axis=0)]
    convert_element_type x1 -> x0, other arithmetic: 4.38 us -> none  [per_device(): jnp.where(observed, (dosage - 2.0 * freq) * scale, 0.0).astype(jnp.bfloat16)]
  transfers between devices with their start and end apart: 2 -> 0, of which waited for: 2 -> 0; matrix products, arithmetic and copies ran while one was open for 0% -> 0% of each run, Pallas kernels for 0% -> 0%
where the time goes in v1:
time: 53.7 us; the launch traced here: 53.5 us
  Pallas kernels  50.6 us (94%)
  local copies, waits for them, and re-layouts  2.27 us (4%)
  between operations  0.65 us (1%)
    pallas_call x1, Pallas kernels, fused(): pl.pallas_call(functools.partial(kernel, n), out_shape=(jax.ShapeDtypeStr...  50.6 us
    unnamed x4, local copies, waits for them, and re-layouts  2.27 us

profile of v1, /device:TPU:0, one launch (start us, length us, event | category | flops | bytes accessed | tf_op | source)
XLA Modules:
  0.0 53.5 jit_solution(5994529808551159876)
XLA Ops:
  0.6 0.0 copy-start
  0.6 0.9 %copy-done = bf16[2048,40]{0,1:T(8,128)(2,1)S(1)} copy-done((bf16[2048,40]{0,1:T(8,128)(2,1)S(1)}, bf16[2048,40]{0,1:T(8,128)(2,1)}, u32[]{:S(2)}) %copy-start) | copy-done | bytes 163864
  1.5 50.6 %shard_map.41 = (bf16[40,1024]{1,0:T(8,128)(2,1)S(1)}, f32[40,2048]{1,0:T(8,128)S(1)}) custom-call(s32[1024,2048]{1,0:T(8,128)} %genotype.1, bf16[40,2048]{1,0:T(8,128)(2,1)S(1)} %bitcast.4), custom_call_target="tpu_custom_call" | custom-call | tf_op jit(solution)/shard_map/pallas_call | solution.py:228
  52.2 0.6 %copy.6 = bf16[1024,40]{0,1:T(8,128)(2,1)} copy(bf16[1024,40]{0,1:T(8,128)(2,1)S(1)} %bitcast.5) | data formatting | bytes 163840
  52.8 0.7 %copy.7 = f32[2048,40]{0,1:T(8,128)} copy(f32[2048,40]{0,1:T(8,128)S(1)} %bitcast.3) | data formatting | bytes 655360
Async XLA Ops:
  0.6 0.9 %copy-start = (bf16[2048,40]{0,1:T(8,128)(2,1)S(1)}, bf16[2048,40]{0,1:T(8,128)(2,1)}, u32[]{:S(2)}) copy-start(bf16[2048,40]{0,1:T(8,128)(2,1)} %param.3) | copy-start | bytes 491524

commit v2 on v1

--- a/solution.py
+++ b/solution.py
@@ -26,7 +26,7 @@
 
 def kernel(
     n, genotype, basis, scores_out, block_out,
-    raw, std, stat, table, start, acc, mine, theirs, part, got, full, result,
+    raw, std, hot, stat, table, start, acc, mine, theirs, part, got, full, result,
     load_sem, in_sem, stat_send, stat_recv, score_send, score_recv,
     part_send, part_recv, full_send, full_recv, out_sem,
 ):
@@ -43,24 +43,21 @@
         pl.semaphore_signal(barrier, inc=1, device_id={"samp": flipped(me, d)}, device_id_type=MESH)
     pl.semaphore_signal(barrier, inc=1, device_id={"snp": 1 - side}, device_id_type=MESH)
 
-    def load(c):
-        at = pl.ds(pl.multiple_of(c * WIDE, WIDE), WIDE)
-        return pltpu.make_async_copy(genotype.at[:, at], raw.at[:, at], load_sem.at[c])
-
-    for c in range(chunks):
+    def load(j):
+        at = pl.ds(pl.multiple_of(j * LANES, LANES), LANES)
+        return pltpu.make_async_copy(genotype.at[:, at], raw.at[j], load_sem.at[j])
+
+    for c in range(blocks):
         load(c).start()
     fetch = pltpu.make_async_copy(basis, start, in_sem)
     fetch.start()
 
-    def count(c, _):
-        load(c).wait()
-        for half in range(WIDE // LANES):
-            at = pl.ds(pl.multiple_of(c * WIDE + half * LANES, LANES), LANES)
-            g = raw[:, at]
-            sums = jnp.sum(jnp.where(g == 3, SHIFT, g), axis=0, keepdims=True)
-            std[:, at] = g.astype(jnp.float32).astype(jnp.bfloat16)
-            j = c * (WIDE // LANES) + half
-            stat[me, j // 8, pl.ds(lax.rem(j, 8), 1), :] = sums
+    def count(j, _):
+        load(j).wait()
+        g = raw[j]
+        sums = jnp.sum(jnp.where(g == 3, SHIFT, g), axis=0, keepdims=True)
+        std[j] = g.astype(jnp.float32).astype(jnp.bfloat16)
+        stat[me, j // 8, pl.ds(lax.rem(j, 8), 1), :] = sums
         return 0
 
     def stat_copy(h, d):
@@ -71,13 +68,23 @@
             device_id={"samp": peer}, device_id_type=MESH,
         )
 
-    per_group = chunks // groups
+    per_group = blocks // groups
     for h in range(groups):
         lax.fori_loop(h * per_group, (h + 1) * per_group, count, 0)
         if h == 0:
             pl.semaphore_wait(barrier, n)
         for d in reversed(range(1, n)):
             stat_copy(h, d).start()
+
+    def planes(j, _):
+        g = std[j]
+        one, two, three, none = (jnp.full(g.shape, v, jnp.bfloat16) for v in (1, 2, 3, 0))
+        hot[0, j] = jnp.maximum(one - g, none)
+        hot[1, j] = jnp.minimum(g, jnp.maximum(two - g, none))
+        hot[2, j] = jnp.maximum(jnp.minimum(g - one, three - g), none)
+        return 0
+
+    lax.fori_loop(0, blocks, planes, 0)
 
     for h in range(groups):
         for d in range(1, n):
@@ -94,20 +101,15 @@
             table[k, h] = (float(k) - 2.0 * freq) * scale
 
     fetch.wait()
-    zero = jnp.zeros((), jnp.bfloat16)
 
     def standardize(j):
-        at = pl.ds(pl.multiple_of(j * LANES, LANES), LANES)
-        g = std[:, at]
         row = [
-            jnp.broadcast_to(
-                table[k, j // 8, pl.ds(lax.rem(j, 8), 1), :].astype(jnp.bfloat16), g.shape
-            )
-            for k in range(3)
+            table[k, j // 8, pl.ds(lax.rem(j, 8), 1), :].astype(jnp.bfloat16) for k in range(3)
         ]
-        std[:, at] = jnp.where(
-            g == 0, row[0], jnp.where(g == 1, row[1], jnp.where(g == 2, row[2], zero))
-        )
+        std[j] = hot[0, j] * row[0] + hot[1, j] * row[1] + hot[2, j] * row[2]
+
+    def pair(c):
+        return jnp.concatenate([std[2 * c], std[2 * c + 1]], axis=1)
 
     acc[...] = jnp.zeros_like(acc)
 
@@ -115,11 +117,12 @@
         for half in range(WIDE // LANES):
             standardize(c * (WIDE // LANES) + half)
         at = pl.ds(pl.multiple_of(c * WIDE, WIDE), WIDE)
-        acc[...] += lax.dot_general(start[:, at], std[:, at], NT, preferred_element_type=jnp.float32)
+        acc[...] += lax.dot_general(start[:, at], pair(c), NT, preferred_element_type=jnp.float32)
         return 0
 
     lax.fori_loop(0, chunks, first, 0)
 
+    sent = []
     for step in range(ITERS):
         last = step == ITERS - 1
         mine[step] = acc[...].astype(jnp.bfloat16)
@@ -136,7 +139,7 @@
             score_write = pltpu.make_async_copy(result, scores_out, out_sem.at[0])
             score_write.start()
 
-        def part_copy(owner):
+        def part_copy(owner, step=step):
             return pltpu.make_async_remote_copy(
                 src_ref=part.at[step, owner], dst_ref=got.at[step, me],
                 send_sem=part_send.at[step, owner], recv_sem=part_recv.at[step, me],
@@ -155,8 +158,8 @@
 
         def back(i, _):
             c = lax.rem(me // per_dot + 1 + i, dots)
-            at = pl.ds(pl.multiple_of(c * (per_dot * LANES), per_dot * LANES), per_dot * LANES)
-            local = jnp.dot(result[...], std[:, at], preferred_element_type=jnp.float32)
+            wide = jnp.concatenate([std[c * per_dot + r] for r in range(per_dot)], axis=1)
+            local = jnp.dot(result[...], wide, preferred_element_type=jnp.float32)
             for r in range(per_dot):
                 owner = c * per_dot + r
                 part[step, owner] = local[:, r * LANES : (r + 1) * LANES].astype(jnp.bfloat16)
@@ -176,7 +179,7 @@
             whole += got[step, sender].astype(jnp.float32)
         full[step, me] = (whole / total).astype(jnp.bfloat16)
 
-        def full_copy(peer, slot):
+        def full_copy(peer, slot, step=step):
             return pltpu.make_async_remote_copy(
                 src_ref=full.at[step, slot], dst_ref=full.at[step, slot],
                 send_sem=full_send.at[step, peer], recv_sem=full_recv.at[step, slot],
@@ -203,17 +206,19 @@
             if last:
                 block_out[:, at] = both.astype(jnp.float32)
             else:
-                acc[...] += lax.dot_general(both, std[:, at], NT, preferred_element_type=jnp.float32)
+                acc[...] += lax.dot_general(both, pair(c), NT, preferred_element_type=jnp.float32)
             return 0
 
         lax.fori_loop(0, n // 2, take, 0)
 
+        sent.append((step, swap))
+
+    for step, swap in sent:
         for d in range(1, n):
             peer = flipped(me, d)
-            part_copy(peer).wait_send()
-            full_copy(peer, me).wait_send()
+            part_copy(peer, step).wait_send()
+            full_copy(peer, me, step).wait_send()
         swap.wait_send()
-
     for h in range(groups):
         for d in range(1, n):
             stat_copy(h, d).wait_send()
@@ -231,14 +236,15 @@
             jax.ShapeDtypeStruct((width, rows), jnp.bfloat16),
             jax.ShapeDtypeStruct((width, cols), jnp.float32),
         ),
-        in_specs=[pl.BlockSpec(memory_space=pl.ANY)] * 2,
+        in_specs=[pl.BlockSpec(memory_space=pltpu.HBM)] * 2,
         out_specs=(
             pl.BlockSpec(memory_space=pl.ANY),
             pl.BlockSpec(memory_space=pltpu.VMEM),
         ),
         scratch_shapes=[
-            pltpu.VMEM((rows, cols), jnp.int32),
-            pltpu.VMEM((rows, cols), jnp.bfloat16),
+            pltpu.VMEM((blocks, rows, LANES), jnp.int32),
+            pltpu.VMEM((blocks, rows, LANES), jnp.bfloat16),
+            pltpu.VMEM((3, blocks, rows, LANES), jnp.bfloat16),
             pltpu.VMEM((n, blocks // 8, 8, LANES), jnp.int32),
             pltpu.VMEM((3, blocks // 8, 8, LANES), jnp.float32),
             pltpu.VMEM((width, cols), jnp.bfloat16),
@@ -249,7 +255,7 @@
             pltpu.VMEM((ITERS, n, width, LANES), jnp.bfloat16),
             pltpu.VMEM((ITERS, n, width, LANES), jnp.bfloat16),
             pltpu.VMEM((width, rows), jnp.bfloat16),
-            dma((cols // WIDE,)),
+            dma((blocks,)),
             dma,
             dma((blocks // 8, n)),
             dma((blocks // 8, n)),

time: 53.7 us -> 49.5 us (0.922)
  Pallas kernels: 50.6 us -> 46.4 us
    pallas_call x1, Pallas kernels: 50.6 us -> 46.4 us  [fused(): pl.pallas_call(functools.partial(kernel, n), out_shape=(jax.ShapeDtypeStr...]
where the time goes in v2:
time: 49.5 us; the launch traced here: 49.4 us
  Pallas kernels  46.4 us (94%)
  local copies, waits for them, and re-layouts  2.27 us (5%)
  between operations  0.65 us (1%)
    pallas_call x1, Pallas kernels, fused(): pl.pallas_call(functools.partial(kernel, n), out_shape=(jax.ShapeDtypeStr...  46.4 us
    unnamed x4, local copies, waits for them, and re-layouts  2.27 us

profile of v2, /device:TPU:0, one launch (start us, length us, event | category | flops | bytes accessed | tf_op | source)
XLA Modules:
  0.0 49.4 jit_solution(12694340582552520845)
XLA Ops:
  0.6 0.0 copy-start
  0.6 0.9 %copy-done = bf16[2048,40]{0,1:T(8,128)(2,1)S(1)} copy-done((bf16[2048,40]{0,1:T(8,128)(2,1)S(1)}, bf16[2048,40]{0,1:T(8,128)(2,1)}, u32[]{:S(2)}) %copy-start) | copy-done | bytes 163864
  1.5 46.4 %shard_map.41 = (bf16[40,1024]{1,0:T(8,128)(2,1)S(1)}, f32[40,2048]{1,0:T(8,128)S(1)}) custom-call(s32[1024,2048]{1,0:T(8,128)} %genotype.1, bf16[40,2048]{1,0:T(8,128)(2,1)S(1)} %bitcast.4), custom_call_target="tpu_custom_call" | custom-call | tf_op jit(solution)/shard_map/pallas_call | solution.py:233
  48.0 0.6 %copy.6 = bf16[1024,40]{0,1:T(8,128)(2,1)} copy(bf16[1024,40]{0,1:T(8,128)(2,1)S(1)} %bitcast.5) | data formatting | bytes 163840
  48.6 0.7 %copy.7 = f32[2048,40]{0,1:T(8,128)} copy(f32[2048,40]{0,1:T(8,128)S(1)} %bitcast.3) | data formatting | bytes 655360
Async XLA Ops:
  0.6 0.9 %copy-start = (bf16[2048,40]{0,1:T(8,128)(2,1)S(1)}, bf16[2048,40]{0,1:T(8,128)(2,1)}, u32[]{:S(2)}) copy-start(bf16[2048,40]{0,1:T(8,128)(2,1)} %param.3) | copy-start | bytes 491524
